TPU v7x, 32 devices: a whole 2x2x4 slice. The times are simulated.
32 devices in a mesh: rep: 8 (over y, x, core), tp: 4 (over z).
Axes of the slice: x: 2, y: 2, z: 4, core: 2. Of those that a mesh axis runs over, the one named last changes fastest.
Arguments:
- residual_in: bfloat16 [8, 512, 8192], P('rep', 'tp'), may hold values from -6 to 6
- norm_gain: bfloat16 [8192], replicated, may hold values from 0.099609375 to 1.8984375
- w_query: bfloat16 [8192, 4096], P(None, 'tp'), may hold values from -1 to 1
- w_keyval: bfloat16 [8192, 1024], P(None, 'tp'), may hold values from -0.0625 to 0.0625
- w_out: bfloat16 [4096, 8192], P('tp'), may hold values from -0.375 to 0.375
- score_head: bfloat16 [8192], replicated, may hold values from -0.0625 to 0.0625
- lengths: int32 [8], P('rep'), may hold values from 256 to 512
- policy_slots: bfloat16 [8, 768, 8192], P('rep', None, 'tp'), may hold values from -6 to 6
Outputs:
- scored_hidden: bfloat16 [8, 512, 8192], P('rep', 'tp')
- rewards: float32 [8], P('rep')
- policy_copies: bfloat16 [8, 768, 8192], P('rep', None, 'tp')
All inputs are finite; a program needn't handle non-finite values.
Results may differ from a plain program's by a relative error of at most 0.017.
The roundings to bfloat16 on the way count: a program that leaves them out, or rounds other values in their place, can miss the bound.
Values may be sent and summed in bfloat16 or wider, within the bound.
A program may use at most 128 MiB of HBM per device.

v0:
```python
import functools

import jax
import jax.numpy as jnp
from jax import lax
from jax.experimental import pallas as pl
from jax.experimental.pallas import tpu as pltpu
from jax.sharding import PartitionSpec as P

QH = 32
KVH = 4
HS = 128
MESH = pl.DeviceIdType.MESH
F32 = jnp.float32
BF16 = jnp.bfloat16
CHUNKS = 8
LAG = 3
DEPTH = 6
GO = 0


def kernel(
    n, R, kvw, heads,
    resid_h, gain, wq_h, wkv_h, wo_h, head, lens, pol_in,
    out_h, rew, pol_out,
    wq, wkv, wo, resid, nrm, part, qs, accq, acckv, kvown, kvin, kf, vf, att, rmy, rin,
    load_sem, ag_send, ag_recv, rs_send, rs_recv, kv_send, kv_recv, r_send, r_recv, p_send, p_recv, p_loc, out_sem, go_sem,
):
    t = lax.axis_index("tp")
    r = lax.axis_index("rep")
    C = nrm.shape[1]
    rows, cols = nrm.shape[2], nrm.shape[3]
    seq = n * rows
    length = lens[0]

    def chunk_of(ref, c):
        return ref.at[:, pl.ds(pl.multiple_of(c * cols, cols), cols)]

    loads = [pltpu.make_async_copy(chunk_of(resid_h.at[0], c), resid.at[c], load_sem.at[c]) for c in range(C)]
    wloads = [
        pltpu.make_async_copy(wq_h, wq, load_sem.at[C]),
        pltpu.make_async_copy(wkv_h, wkv, load_sem.at[C + 1]),
    ]
    oloads = [pltpu.make_async_copy(chunk_of(wo_h, c), wo.at[c], load_sem.at[C + 2 + c]) for c in range(C)]
    for cp in loads + wloads + oloads:
        cp.start()
    kf[...] = jnp.zeros_like(kf)
    vf[...] = jnp.zeros_like(vf)

    barrier = pltpu.get_barrier_semaphore()
    for k in range(1, n):
        pl.semaphore_signal(barrier, inc=1, device_id={"tp": lax.rem(t + k, n)}, device_id_type=MESH)
    for k in range(1, R):
        pl.semaphore_signal(barrier, inc=1, device_id={"rep": lax.rem(r + k, R)}, device_id_type=MESH)

    for cp in loads:
        cp.wait()

    def sq(c, acc):
        x = resid[c].astype(F32)
        return acc + jnp.sum(x * x, axis=1, keepdims=True)

    ms = lax.fori_loop(0, C, sq, jnp.zeros((rows, 1), F32))
    scale = lax.rsqrt(ms / (C * cols) + 1e-05)

    def norm(c, carry):
        nrm[t, c] = (resid[c].astype(F32) * scale * gain[c].astype(F32)).astype(BF16)
        return carry

    lax.fori_loop(0, C, norm, 0)
    pl.semaphore_wait(barrier, n - 1 + R - 1)

    steps = R.bit_length() - 1

    def pol(src, s):
        return pltpu.make_async_remote_copy(
            src, pol_out, p_send.at[s], p_recv, device_id={"rep": r + (R >> (s + 1))}, device_id_type=MESH
        )

    @pl.when(r == 0)
    def _():
        for s in range(steps):
            pol(pol_in, s).start()
        pltpu.make_async_copy(pol_in, pol_out, p_loc).start()

    def pol_point(s):
        gap = R >> (s + 1)

        @pl.when(lax.rem(r, 2 * gap) == gap)
        def _():
            pltpu.make_async_copy(pol_out, pol_out, p_recv).wait()
            for q in range(s + 1, steps):
                pol(pol_out, q).start()

    def ag_copy(d, b, c, slot):
        return pltpu.make_async_remote_copy(
            nrm.at[b, c], nrm.at[b, c], ag_send.at[d, slot], ag_recv.at[b, c],
            device_id={"tp": t + (1 if d == 0 else -1)}, device_id_type=MESH,
        )

    def ag_wait(b, c):
        pltpu.make_async_copy(nrm.at[b, c], nrm.at[b, c], ag_recv.at[b, c]).wait()

    def ag_up(i):
        old = i - DEPTH
        jo = jnp.maximum(old, 0) // C

        @pl.when((old >= 0) & (jo <= t) & (t < n - 1))
        def _():
            ag_copy(0, jo, lax.rem(old, C), lax.rem(i, DEPTH)).wait_send()

        j = jnp.maximum(i, 0) // C
        c = lax.rem(jnp.maximum(i, 0), C)

        @pl.when((i >= 0) & (j < t))
        def _():
            ag_wait(j, c)

        @pl.when((i >= 0) & (j <= t) & (t < n - 1))
        def _():
            ag_copy(0, j, c, lax.rem(i, DEPTH)).start()

    def ag_down(i):
        old = i - DEPTH
        bo = t + jnp.maximum(old, 0) // C

        @pl.when((old >= 0) & (bo < n) & (t > 0))
        def _():
            ag_copy(1, bo, lax.rem(jnp.maximum(old, 0), C), lax.rem(i, DEPTH)).wait_send()

        b = t + i // C
        c = lax.rem(i, C)

        @pl.when((b < n) & (t > 0))
        def _():
            @pl.when(b > t)
            def _():
                ag_wait(b, c)

            ag_copy(1, b, c, lax.rem(i, DEPTH)).start()

    def rs_copy(d, b, c, slot):
        dst = b if d == 0 else jnp.where(b == t - 1, n, b)
        return pltpu.make_async_remote_copy(
            part.at[b, c], part.at[dst, c], rs_send.at[d, slot], rs_recv.at[dst, c],
            device_id={"tp": t + (1 if d == 0 else -1)}, device_id_type=MESH,
        )

    def rs_wait(slot, c):
        pltpu.make_async_copy(part.at[slot, c], part.at[slot, c], rs_recv.at[slot, c]).wait()

    def project(b, c):
        return jnp.dot(att[b], wo[c], preferred_element_type=F32).astype(BF16)

    def rs_step(d, i):
        first = 1 if d == 0 else 0

        def live(b):
            return (b < n) & ((b > t) if d == 0 else (b < t))

        old = i - DEPTH
        bo = first + jnp.maximum(old, 0) // C

        @pl.when((old >= 0) & live(bo))
        def _():
            rs_copy(d, bo, lax.rem(jnp.maximum(old, 0), C), lax.rem(i, DEPTH)).wait_send()

        b = first + jnp.maximum(i, 0) // C
        c = lax.rem(jnp.maximum(i, 0), C)
        has = (t > 0) if d == 0 else (t < n - 1)

        @pl.when((i >= 0) & live(b))
        def _():
            mine = project(b, c)

            @pl.when(has)
            def _():
                rs_wait(b, c)
                part[b, c] = (part[b, c].astype(F32) + mine.astype(F32)).astype(BF16)

            @pl.when(jnp.logical_not(has))
            def _():
                part[b, c] = mine

            rs_copy(d, b, c, lax.rem(i, DEPTH)).start()

    group = QH // KVH
    pieces = kvw // HS
    my_head = (t * heads) // group

    def kv_copy(b, p, k):
        target = lax.rem(t + k, n)
        gid = t * pieces + p
        is_v = gid // KVH
        return target, gid, pltpu.make_async_remote_copy(
            kvown.at[p], kvin.at[b, is_v], kv_send.at[p, k], kv_recv.at[b, is_v],
            device_id={"tp": target}, device_id_type=MESH,
        )

    def compute_block(b):
        if b > 0:
            @pl.when(t == 0)
            def _():
                for c in range(C):
                    ag_wait(b, c)

        if b == 0:
            for cp in wloads:
                cp.wait()
        accq[...] = jnp.zeros_like(accq)
        acckv[...] = jnp.zeros_like(acckv)

        def mm(c, carry):
            x = nrm[b, c]
            acckv[...] += jnp.dot(x, wkv[c], preferred_element_type=F32)
            accq[...] += jnp.dot(x, wq[c], preferred_element_type=F32)
            return carry

        lax.fori_loop(0, C, mm, 0)
        for p in range(pieces):
            kvown[p] = acckv[:, p * HS : (p + 1) * HS].astype(BF16)
        for p in range(pieces):
            gid = t * pieces + p
            for k in range(1, n):
                target, _, cp = kv_copy(b, p, k)

                @pl.when(lax.rem(gid, KVH) == (target * heads) // group)
                def _(cp=cp):
                    cp.start()

            here = lax.rem(gid, KVH) == my_head

            @pl.when(here & (gid < KVH))
            def _(p=p):
                kf[b * rows : (b + 1) * rows, :] = kvown[p]

            @pl.when(here & (gid >= KVH))
            def _(p=p):
                vf[b * rows : (b + 1) * rows, :] = kvown[p]

        for h in range(heads):
            qs[h] = accq[:, h * HS : (h + 1) * HS].astype(BF16)
        for is_v, full in ((0, kf), (1, vf)):
            owner = (is_v * KVH + my_head) // pieces

            @pl.when(owner != t)
            def _(is_v=is_v, full=full):
                pltpu.make_async_copy(kvin.at[b, is_v], kvin.at[b, is_v], kv_recv.at[b, is_v]).wait()
                full[b * rows : (b + 1) * rows, :] = kvin[b, is_v]

        span = (b + 1) * rows
        rowpos = b * rows + lax.broadcasted_iota(jnp.int32, (rows, span), 0)
        colpos = lax.broadcasted_iota(jnp.int32, (rows, span), 1)
        valid = (colpos <= rowpos) & (colpos < length)
        for h in range(heads):
            s = lax.dot_general(
                qs[h], kf[:span, :], (((1,), (1,)), ((), ())), preferred_element_type=F32
            ) * HS ** (-0.5)
            s = jnp.where(valid, s, -1e30)
            e = jnp.exp(s - jnp.max(s, axis=1, keepdims=True))
            pr = (e / jnp.sum(e, axis=1, keepdims=True)).astype(BF16)
            att[b, :, h * HS : (h + 1) * HS] = jnp.dot(
                pr, vf[:span, :], preferred_element_type=F32
            ).astype(BF16)
        for p in range(pieces):
            gid = t * pieces + p
            for k in range(1, n):
                target, _, cp = kv_copy(b, p, k)

                @pl.when(lax.rem(gid, KVH) == (target * heads) // group)
                def _(cp=cp):
                    cp.wait_send()

    skew = (n - 1) * LAG
    marks = [(j + 1) * C + skew for j in range(n - 1)]
    up_end = marks[min(1, n - 2)] + (n - 1) * C + skew + DEPTH
    down_end = marks[0] + (n - 1) * C + skew + DEPTH
    up_base = marks[min(1, n - 2)]

    def ag(k):
        ag_down(k)
        ag_up(k - t * LAG)

    def rs_d(k):
        rs_step(1, k - marks[0] - (n - 1 - t) * LAG)

    def rs_u(k):
        rs_step(0, k - up_base - t * LAG)

    def run(lo, hi, fs):
        def body(k, carry):
            for f in fs:
                f(k)
            return carry

        if hi > lo:
            lax.fori_loop(lo, hi, body, 0)

    @pl.when(lax.rem(r, 2) == 1)
    def _():
        pl.semaphore_wait(go_sem, 1)

    run(0, marks[0], [ag])
    for b in range(n):
        if b == min(GO, n - 1):
            @pl.when(lax.rem(r, 2) == 0)
            def _():
                pl.semaphore_signal(go_sem, inc=1, device_id={"rep": r + 1}, device_id_type=MESH)

        compute_block(b)
        if b < steps - 1:
            pol_point(b)
        if b == 0:
            for cp in oloads:
                cp.wait()
        if b < n - 2:
            fs = [ag, rs_d]
            if b >= 1:
                fs.append(rs_u)
            run(marks[b], marks[b + 1], fs)
    for s in range(n, steps - 1):
        pol_point(s)
    top = marks[n - 2]
    run(top, top + DEPTH, [ag, rs_u, rs_d])
    run(top + DEPTH, max(up_end, down_end), [rs_u, rs_d])

    local_last = length - 1 - t * rows
    rowid = lax.broadcasted_iota(jnp.int32, (rows, 1), 0)
    weight = jnp.where(rowid == local_last, 1.0, 0.0) + seq ** (-0.5)

    def fin(c, acc):
        total = project(t, c).astype(F32)

        @pl.when(t > 0)
        def _():
            rs_wait(t, c)

        @pl.when(t < n - 1)
        def _():
            rs_wait(n, c)

        below = jnp.where(t > 0, part[t, c].astype(F32), 0.0)
        above = jnp.where(t < n - 1, part[n, c].astype(F32), 0.0)
        hid = (resid[c].astype(F32) + (total + below + above)).astype(BF16)
        resid[c] = hid
        pltpu.make_async_copy(resid.at[c], chunk_of(out_h.at[0], c), out_sem.at[c]).start()
        return acc + jnp.sum(hid.astype(F32) * head[c].astype(F32), axis=1, keepdims=True)

    score = lax.fori_loop(0, C, fin, jnp.zeros((rows, 1), F32))
    rmy[...] = jnp.broadcast_to(jnp.sum(score * weight, keepdims=True), rmy.shape)
    pol_point(steps - 1)

    def rcopy(k):
        return pltpu.make_async_remote_copy(
            rmy, rin.at[k - 1], r_send.at[k - 1], r_recv.at[k - 1],
            device_id={"tp": lax.rem(t + k, n)}, device_id_type=MESH,
        )

    for k in range(1, n):
        rcopy(k).start()
    total = rmy[...]
    for k in range(1, n):
        rcopy(k).wait()
        total = total + rin[k - 1]
    rew[...] = total
    for c in range(C):
        pltpu.make_async_copy(resid.at[c], chunk_of(out_h.at[0], c), out_sem.at[c]).wait()

    @pl.when(r == 0)
    def _():
        for s in range(steps):
            pol(pol_in, s).wait_send()
        pltpu.make_async_copy(pol_in, pol_out, p_loc).wait()

    for s in range(steps - 1):
        gap = R >> (s + 1)

        @pl.when(lax.rem(r, 2 * gap) == gap)
        def _(s=s):
            for q in range(s + 1, steps):
                pol(pol_out, q).wait_send()


def solution(mesh):
    n, R = mesh.shape["tp"], mesh.shape["rep"]

    def on_device(residual_in, norm_gain, w_query, w_keyval, w_out, score_head, lengths, policy_slots):
        rows, width = residual_in.shape[1:]
        qw, kvw = w_query.shape[1], w_keyval.shape[1]
        heads = qw // HS
        C = CHUNKS
        cols = width // C
        sem = pltpu.SemaphoreType.DMA
        vm = pl.BlockSpec(memory_space=pltpu.VMEM)
        hbm = pl.BlockSpec(memory_space=pl.ANY)
        hidden, reward, policy = pl.pallas_call(
            functools.partial(kernel, n, R, kvw, heads),
            out_shape=(
                jax.ShapeDtypeStruct(residual_in.shape, BF16),
                jax.ShapeDtypeStruct((8, 128), F32),
                jax.ShapeDtypeStruct(policy_slots.shape, BF16),
            ),
            in_specs=[hbm, vm, hbm, hbm, hbm, vm, pl.BlockSpec(memory_space=pltpu.SMEM), hbm],
            out_specs=(hbm, vm, hbm),
            scratch_shapes=[
                pltpu.VMEM((C, cols, qw), BF16),
                pltpu.VMEM((C, cols, kvw), BF16),
                pltpu.VMEM((C, qw, cols), BF16),
                pltpu.VMEM((C, rows, cols), BF16),
                pltpu.VMEM((n, C, rows, cols), BF16),
                pltpu.VMEM((n + 1, C, rows, cols), BF16),
                pltpu.VMEM((heads, rows, HS), BF16),
                pltpu.VMEM((rows, qw), F32),
                pltpu.VMEM((rows, kvw), F32),
                pltpu.VMEM((kvw // HS, rows, HS), BF16),
                pltpu.VMEM((n, 2, rows, HS), BF16),
                pltpu.VMEM((n * rows, HS), BF16),
                pltpu.VMEM((n * rows, HS), BF16),
                pltpu.VMEM((n, rows, qw), BF16),
                pltpu.VMEM((8, 128), F32),
                pltpu.VMEM((n - 1, 8, 128), F32),
                sem((2 * C + 2,)),
                sem((2, DEPTH)),
                sem((n, C)),
                sem((2, DEPTH)),
                sem((n + 1, C)),
                sem((kvw // HS, n)),
                sem((n, 2)),
                sem((n - 1,)),
                sem((n - 1,)),
                sem((R.bit_length() - 1,)),
                sem,
                sem,
                sem((C,)),
                pltpu.SemaphoreType.REGULAR,
            ],
            compiler_params=pltpu.CompilerParams(
                collective_id=0, has_side_effects=True, vmem_limit_bytes=67043328
            ),
        )(
            residual_in,
            norm_gain.reshape(C, 1, cols),
            w_query.reshape(C, cols, qw),
            w_keyval.reshape(C, cols, kvw),
            w_out,
            score_head.reshape(C, 1, cols),
            lengths,
            policy_slots,
        )
        return hidden, reward[0, :1], policy

    return jax.shard_map(
        on_device,
        mesh=mesh,
        in_specs=(
            P("rep", "tp", None),
            P(),
            P(None, "tp"),
            P(None, "tp"),
            P("tp", None),
            P(),
            P("rep"),
            P("rep", None, "tp"),
        ),
        out_specs=(P("rep", "tp", None), P("rep"), P("rep", None, "tp")),
        check_vma=False,
    )
```

profile of v0, /device:TPU:1, one launch (start us, length us, event | category | flops | bytes accessed | tf_op | source)
XLA Modules:
  0.0 301.1 jit_solution(16084977646111238378)
XLA Ops:
  1.3 1.3 reshape.22.gain
  2.6 1.3 reshape.23.head
  4.0 291.0 %shard_map.103 = (bf16[1,128,8192]{2,1,0:T(8,128)(2,1)}, f32[8,128]{1,0:T(8,128)}, bf16[1,768,2048]{2,1,0:T(8,128)(2,1)}) custom-call(bf16[1,128,8192]{2,1,0:T(8,128)(2,1)} %resid_h.1, bf16[8,1,1024]{2,1,0:T(2,128)(2,1)} %reshape.22.gain, bf16[8,1024,1024]{2,1,0:T(8,128)(2,1)} %bitcast.3, bf16[8,1024,256]{2,1,0:T(8,128)(2,1)} %bitcast.4, ...), custom_call_target="tpu_custom_call" | custom-call | tf_op jit(solution)/shard_map/pallas_call | solution.py:396
  294.9 0.0 copy-start
  295.0 1.3 slice.3
  296.3 3.1 %copy.16 = bf16[1,128,8192]{2,1,0:T(8,128)(2,1)} copy(bf16[1,128,8192]{2,1,0:T(8,128)(2,1)} %get-tuple-element.12) | data formatting | bytes 4194304
  299.4 0.0 copy-done
  299.4 1.7 copy.17
Async XLA Ops:
  294.9 4.4 %copy-start = (bf16[1,768,2048]{2,1,0:T(8,128)(2,1)S(1)}, bf16[1,768,2048]{2,1,0:T(8,128)(2,1)}, u32[]{:S(2)}) copy-start(bf16[1,768,2048]{2,1,0:T(8,128)(2,1)} %get-tuple-element.14) | copy-start | bytes 9437188
where the time goes:
time: 301 us
  Pallas kernels  291 us (97%)
  local copies, waits for them, and re-layouts  8.78 us (3%)
    pallas_call x1, Pallas kernels, on_device(): pl.pallas_call(functools.partial(kernel, n, R, kvw, heads), out_shape=(ja...  291 us

commit v1 on v0

v1 whole, which is shorter than its diff:
```python
import functools

import jax
import jax.numpy as jnp
from jax import lax
from jax.experimental import pallas as pl
from jax.experimental.pallas import tpu as pltpu
from jax.sharding import PartitionSpec as P

QH = 32
KVH = 4
HS = 128
MESH = pl.DeviceIdType.MESH
F32 = jnp.float32
BF16 = jnp.bfloat16
CHUNKS = 8
DEPTH = 3
GO_STEP = 8
GO_LAST = 44
LAG = 2
NEVER = 1 << 20
POL_TICKS = (24, 56)

TUNED = {(4, 8): {(0, 0): dict(up={0: 0}, down={1: 4, 2: 20, 3: 47}, sum_up={1: 31, 2: 47, 3: 74}, sum_down={}, attend={0: 30, 1: 31, 2: 36, 3: 54}, own=1, fin=91), (0, 1): dict(up={0: 22}, down={1: 31, 2: 39, 3: 63}, sum_up={1: 59, 2: 71, 3: 94}, sum_down={}, attend={0: 45, 1: 59, 2: 67, 3: 74}, own=10, fin=97), (1, 0): dict(up={0: 1, 1: 9}, down={1: 0, 2: 9, 3: 21}, sum_up={2: 43, 3: 81}, sum_down={0: 84}, attend={0: 15, 1: 30, 2: 39, 3: 48}, own=14, fin=95), (1, 1): dict(up={0: 21, 1: 29}, down={1: 20, 2: 30, 3: 38}, sum_up={2: 73, 3: 91}, sum_down={0: 71}, attend={0: 37, 1: 41, 2: 70, 3: 80}, own=13, fin=115), (2, 0): dict(up={0: 5, 1: 13, 2: 32}, down={2: 0, 3: 10}, sum_up={3: 72}, sum_down={0: 27, 1: 72}, attend={0: 14, 1: 45, 2: 46, 3: 48}, own=3, fin=65), (2, 1): dict(up={0: 19, 1: 27, 2: 42}, down={2: 20, 3: 28}, sum_up={3: 85}, sum_down={0: 49, 1: 84}, attend={0: 28, 1: 53, 2: 65, 3: 67}, own=6, fin=84), (3, 0): dict(up={0: 6, 1: 18, 2: 31}, down={3: 3}, sum_up={}, sum_down={0: 19, 1: 29, 2: 78}, attend={0: 18, 1: 27, 2: 42, 3: 46}, own=17, fin=112), (3, 1): dict(up={0: 2, 1: 31, 2: 44}, down={3: 0}, sum_up={}, sum_down={0: 28, 1: 60, 2: 72}, attend={0: 24, 1: 49, 2: 60, 3: 76}, own=3, fin=114), }}


def plan(n, C):
    if (n, C) in TUNED:
        return TUNED[(n, C)]
    table = {}
    pad = LAG * (n - 1) + 3
    for t in range(n):
        w = n - 1 - t
        for p in range(2):
            late = p * n * C
            up = {j: late + j * C + LAG * t for j in range(t + 1) if j < n - 1}
            down = {b: late + (b - t) * C + LAG * w for b in range(t, n) if b > 0}
            attend = {b: late + min(b + 1, n - 1) * C + pad + b for b in range(n)}
            sums = late + (n - 1) * C + pad + n
            sum_up = {b: sums + (b - 1) * C + 2 * t for b in range(t + 1, n)}
            sum_down = {b: sums + b * C + 2 * w for b in range(t)}
            table[t, p] = dict(
                up=up, down=down, sum_up=sum_up, sum_down=sum_down, attend=attend,
                own=late + 1, fin=sums + (n - 1) * C + 2 * n,
            )
    return table


def kernel(
    n, R, kvw, heads,
    resid_h, gain, wq_h, wkv_h, wo_h, head, lens, pol_in,
    out_h, rew, pol_out,
    wq, wkv, wo, resid, nrm, part, accq, acckv, kvown, kvin, kf, vf, att, score, rmy, rin,
    load_sem, ag_send, ag_recv, rs_send, rs_recv, kv_send, kv_recv, r_send, r_recv, p_send, p_recv, p_loc, out_sem, go_sem,
):
    t = lax.axis_index("tp")
    r = lax.axis_index("rep")
    par = lax.rem(r, 2)
    C = nrm.shape[1]
    rows, cols = nrm.shape[2], nrm.shape[3]
    seq = n * rows
    length = lens[0]

    def chunk_of(ref, c):
        return ref.at[:, pl.ds(pl.multiple_of(c * cols, cols), cols)]

    loads = [pltpu.make_async_copy(chunk_of(resid_h.at[0], c), resid.at[c], load_sem.at[c]) for c in range(C)]
    wloads = [
        pltpu.make_async_copy(wkv_h, wkv, load_sem.at[C + 1]),
        pltpu.make_async_copy(wq_h, wq, load_sem.at[C]),
    ]
    oloads = [pltpu.make_async_copy(chunk_of(wo_h, c), wo.at[c], load_sem.at[C + 2 + c]) for c in range(C)]
    for cp in loads:
        cp.start()

    barrier = pltpu.get_barrier_semaphore()
    for k in range(1, n):
        pl.semaphore_signal(barrier, inc=1, device_id={"tp": lax.rem(t + k, n)}, device_id_type=MESH)
    for k in range(1, R):
        pl.semaphore_signal(barrier, inc=1, device_id={"rep": lax.rem(r + k, R)}, device_id_type=MESH)

    for cp in loads:
        cp.wait()
    for cp in wloads + oloads:
        cp.start()

    def sq(c, acc):
        x = resid[c].astype(F32)
        return acc + jnp.sum(x * x, axis=1, keepdims=True)

    ms = lax.fori_loop(0, C, sq, jnp.zeros((rows, 1), F32))
    scale = lax.rsqrt(ms / (C * cols) + 1e-05)

    def norm(c, carry):
        nrm[t, c] = (resid[c].astype(F32) * scale * gain[c].astype(F32)).astype(BF16)
        return carry

    lax.fori_loop(0, C, norm, 0)
    pl.semaphore_wait(barrier, n - 1 + R - 1)

    steps = R.bit_length() - 1

    def pol(src, s):
        return pltpu.make_async_remote_copy(
            src, pol_out, p_send.at[s], p_recv, device_id={"rep": r + (R >> (s + 1))}, device_id_type=MESH
        )

    @pl.when(r == 0)
    def _():
        for s in range(steps):
            pol(pol_in, s).start()
        pltpu.make_async_copy(pol_in, pol_out, p_loc).start()

    def pol_point(s):
        gap = R >> (s + 1)

        @pl.when(lax.rem(r, 2 * gap) == gap)
        def _():
            pltpu.make_async_copy(pol_out, pol_out, p_recv).wait()
            for q in range(s + 1, steps):
                pol(pol_out, q).start()

    table = plan(n, C)
    last = 0
    for entry in table.values():
        last = max(last, entry["fin"] + C, GO_LAST + 1)

    def pick(value):
        out = jnp.int32(value(table[0, 0]))
        for (a, p), entry in table.items():
            out = jnp.where((t == a) & (par == p), jnp.int32(value(entry)), out)
        return out

    def starts(name, low, high):
        result = []
        for b in range(n):
            def value(entry, b=b):
                known = entry[name]
                if b in known:
                    return known[b]
                return low if known and b < min(known) else high
            result.append(pick(value))
        return result

    up_at = starts("up", -NEVER, NEVER)
    down_at = starts("down", -NEVER, NEVER)
    sum_up_at = starts("sum_up", -NEVER, NEVER)
    sum_down_at = starts("sum_down", -NEVER, NEVER)
    attend_at = starts("attend", -NEVER, NEVER)
    own_at = pick(lambda e: e["own"])
    fin_at = pick(lambda e: e["fin"])

    def first_mm(e, a):
        return min([e["own"]] + [v for name in ("up", "down") for b, v in e[name].items() if b != a])

    mm_at = jnp.int32(0)
    wo_at = jnp.int32(0)
    for (a, p), e in table.items():
        here = (t == a) & (par == p)
        mm_at = jnp.where(here, jnp.int32(first_mm(e, a)), mm_at)
        wo_at = jnp.where(here, jnp.int32(min([e["fin"]] + list(e["sum_up"].values()) + list(e["sum_down"].values()))), wo_at)

    def at_tick(k, begins):
        j = jnp.int32(-1)
        begin = jnp.int32(NEVER)
        for b in range(n):
            hit = k >= begins[b]
            j = jnp.where(hit, b, j)
            begin = jnp.where(hit, begins[b], begin)
        c = k - begin
        live = (c >= 0) & (c < C)
        return live, jnp.maximum(j, 0), jnp.clip(c, 0, C - 1)

    group = QH // KVH
    pieces = kvw // HS
    my_head = (t * heads) // group

    def kv_copy(b, p, k):
        target = lax.rem(t + k, n)
        gid = t * pieces + p
        is_v = gid // KVH
        return target, gid, pltpu.make_async_remote_copy(
            kvown.at[b, p], kvin.at[b, is_v], kv_send.at[b, p, k - 1], kv_recv.at[b, is_v],
            device_id={"tp": target}, device_id_type=MESH,
        )

    def multiply(b, c):
        x = nrm[b, c]
        acckv[b] += jnp.dot(x, wkv[c], preferred_element_type=F32)
        accq[b] += jnp.dot(x, wq[c], preferred_element_type=F32)

        @pl.when(c == C - 1)
        def _():
            span = pl.ds(pl.multiple_of(b * rows, rows), rows)
            for p in range(pieces):
                kvown[b, p] = acckv[b, :, p * HS : (p + 1) * HS].astype(BF16)
            for p in range(pieces):
                for k in range(1, n):
                    target, gid, cp = kv_copy(b, p, k)

                    @pl.when(lax.rem(gid, KVH) == (target * heads) // group)
                    def _(cp=cp):
                        cp.start()

                gid = t * pieces + p
                here = lax.rem(gid, KVH) == my_head

                @pl.when(here & (gid < KVH))
                def _(p=p):
                    kf[span, :] = kvown[b, p]

                @pl.when(here & (gid >= KVH))
                def _(p=p):
                    vf[span, :] = kvown[b, p]

    def ag_copy(d, b, c, slot):
        return pltpu.make_async_remote_copy(
            nrm.at[b, c], nrm.at[b, c], ag_send.at[d, slot], ag_recv.at[b, c],
            device_id={"tp": t + (1 if d == 0 else -1)}, device_id_type=MESH,
        )

    def ag_step(d, k):
        live, b, c = at_tick(k, up_at if d == 0 else down_at)
        i = (b if d == 0 else b - t) * C + c
        has = (t < n - 1) if d == 0 else (t > 0)

        @pl.when(live & (b != t))
        def _():
            pltpu.make_async_copy(nrm.at[b, c], nrm.at[b, c], ag_recv.at[b, c]).wait()

        @pl.when(live & has)
        def _():
            @pl.when(i >= DEPTH)
            def _():
                ag_copy(d, b, c, lax.rem(i, DEPTH)).wait_send()

            ag_copy(d, b, c, lax.rem(i, DEPTH)).start()

        return live & (b != t), b, c

    def rs_copy(d, b, c, slot):
        dst = b if d == 0 else jnp.where(b == t - 1, n, b)
        return pltpu.make_async_remote_copy(
            part.at[b, c], part.at[dst, c], rs_send.at[d, slot], rs_recv.at[dst, c],
            device_id={"tp": t + (1 if d == 0 else -1)}, device_id_type=MESH,
        )

    def rs_wait(slot, c):
        pltpu.make_async_copy(part.at[slot, c], part.at[slot, c], rs_recv.at[slot, c]).wait()

    def project(b, c):
        return jnp.dot(att[b], wo[c], preferred_element_type=F32).astype(BF16)

    def rs_step(d, k):
        live, b, c = at_tick(k, sum_up_at if d == 0 else sum_down_at)
        i = (b - t - 1 if d == 0 else b) * C + c
        has = (t > 0) if d == 0 else (t < n - 1)

        @pl.when(live)
        def _():
            mine = project(b, c)

            @pl.when(has)
            def _():
                rs_wait(b, c)
                part[b, c] = (part[b, c].astype(F32) + mine.astype(F32)).astype(BF16)

            @pl.when(jnp.logical_not(has))
            def _():
                part[b, c] = mine

            @pl.when(i >= DEPTH)
            def _():
                rs_copy(d, b, c, lax.rem(i, DEPTH)).wait_send()

            rs_copy(d, b, c, lax.rem(i, DEPTH)).start()

    def attend(b):
        span = pl.ds(pl.multiple_of(b * rows, rows), rows)
        for is_v, full in ((0, kf), (1, vf)):
            owner = (is_v * KVH + my_head) // pieces

            @pl.when(owner != t)
            def _(is_v=is_v, full=full):
                pltpu.make_async_copy(kvin.at[b, is_v], kvin.at[b, is_v], kv_recv.at[b, is_v]).wait()
                full[span, :] = kvin[b, is_v]

        rowpos = b * rows + lax.broadcasted_iota(jnp.int32, (rows, seq), 0)
        colpos = lax.broadcasted_iota(jnp.int32, (rows, seq), 1)
        valid = (colpos <= rowpos) & (colpos < length)
        for h in range(heads):
            s = lax.dot_general(
                accq[b, :, h * HS : (h + 1) * HS].astype(BF16), kf[...],
                (((1,), (1,)), ((), ())), preferred_element_type=F32,
            ) * HS ** (-0.5)
            s = jnp.where(valid, s, -1e30)
            e = jnp.exp(s - jnp.max(s, axis=1, keepdims=True))
            pr = (e / jnp.sum(e, axis=1, keepdims=True)).astype(BF16)
            att[b, :, h * HS : (h + 1) * HS] = jnp.dot(
                pr, vf[...], preferred_element_type=F32
            ).astype(BF16)

    def fin(c):
        total = project(t, c).astype(F32)

        @pl.when(t > 0)
        def _():
            rs_wait(t, c)

        @pl.when(t < n - 1)
        def _():
            rs_wait(n, c)

        below = jnp.where(t > 0, part[t, c].astype(F32), 0.0)
        above = jnp.where(t < n - 1, part[n, c].astype(F32), 0.0)
        hid = (resid[c].astype(F32) + (total + below + above)).astype(BF16)
        resid[c] = hid
        pltpu.make_async_copy(resid.at[c], chunk_of(out_h.at[0], c), out_sem.at[c]).start()
        weighed = hid.astype(F32) * head[c].astype(F32)
        acc = score[...]
        for q in range(cols // HS):
            acc = acc + weighed[:, q * HS : (q + 1) * HS]
        score[...] = acc

    def zero():
        kf[...] = jnp.zeros_like(kf)
        vf[...] = jnp.zeros_like(vf)
        score[...] = jnp.zeros_like(score)
        for b in range(n):
            accq[b] = jnp.zeros(accq.shape[1:], F32)
            acckv[b] = jnp.zeros(acckv.shape[1:], F32)

    def tick(k, carry):
        @pl.when((lax.rem(k, GO_STEP) == 0) & (k > 0) & (k <= GO_LAST))
        def _():
            @pl.when(par == 0)
            def _():
                pl.semaphore_signal(go_sem, inc=1, device_id={"rep": r + 1}, device_id_type=MESH)

            @pl.when(par == 1)
            def _():
                pl.semaphore_wait(go_sem, 1)

        @pl.when(k == mm_at)
        def _():
            zero()
            for cp in wloads:
                cp.wait()

        @pl.when(k == wo_at)
        def _():
            for cp in oloads:
                cp.wait()

        for d in (0, 1):
            live, b, c = ag_step(d, k)

            @pl.when(live)
            def _(b=b, c=c):
                multiply(b, c)

        own = k - own_at

        @pl.when((own >= 0) & (own < C))
        def _():
            multiply(t, jnp.clip(own, 0, C - 1))

        due = jnp.int32(-1)
        for b in range(n):
            due = jnp.where(k == attend_at[b], b, due)

        @pl.when(due >= 0)
        def _():
            attend(jnp.maximum(due, 0))

        for s in range(steps - 1):
            @pl.when(k == POL_TICKS[min(s, len(POL_TICKS) - 1)] + s)
            def _(s=s):
                pol_point(s)

        rs_step(0, k)
        rs_step(1, k)
        f = k - fin_at

        @pl.when((f >= 0) & (f < C))
        def _():
            fin(jnp.clip(f, 0, C - 1))

        return carry

    lax.fori_loop(0, last, tick, 0)

    local_last = length - 1 - t * rows
    rowid = lax.broadcasted_iota(jnp.int32, (rows, 1), 0)
    weight = jnp.where(rowid == local_last, 1.0, 0.0) + seq ** (-0.5)
    rmy[...] = jnp.broadcast_to(jnp.sum(score[...] * weight, keepdims=True), rmy.shape)

    def rcopy(k):
        return pltpu.make_async_remote_copy(
            rmy, rin.at[k - 1], r_send.at[k - 1], r_recv.at[k - 1],
            device_id={"tp": lax.rem(t + k, n)}, device_id_type=MESH,
        )

    for k in range(1, n):
        rcopy(k).start()
    pol_point(steps - 1)

    for d in (0, 1):
        has = (t < n - 1) if d == 0 else (t > 0)

        @pl.when(has)
        def _(d=d):
            for q in range(DEPTH):
                ag_copy(d, t, 0, q).wait_send()
                rs_copy(d, t, 0, q).wait_send()

    def kv_drain(b, carry):
        for p in range(pieces):
            for k in range(1, n):
                target, gid, cp = kv_copy(b, p, k)

                @pl.when(lax.rem(gid, KVH) == (target * heads) // group)
                def _(cp=cp):
                    cp.wait_send()
        return carry

    lax.fori_loop(0, n, kv_drain, 0)

    total = rmy[...]
    for k in range(1, n):
        rcopy(k).wait()
        total = total + rin[k - 1]
    rew[...] = total
    for c in range(C):
        pltpu.make_async_copy(resid.at[c], chunk_of(out_h.at[0], c), out_sem.at[c]).wait()

    @pl.when(r == 0)
    def _():
        for s in range(steps):
            pol(pol_in, s).wait_send()
        pltpu.make_async_copy(pol_in, pol_out, p_loc).wait()

    for s in range(steps - 1):
        gap = R >> (s + 1)

        @pl.when(lax.rem(r, 2 * gap) == gap)
        def _(s=s):
            for q in range(s + 1, steps):
                pol(pol_out, q).wait_send()


def solution(mesh):
    n, R = mesh.shape["tp"], mesh.shape["rep"]

    def on_device(residual_in, norm_gain, w_query, w_keyval, w_out, score_head, lengths, policy_slots):
        rows, width = residual_in.shape[1:]
        qw, kvw = w_query.shape[1], w_keyval.shape[1]
        heads = qw // HS
        C = CHUNKS
        cols = width // C
        sem = pltpu.SemaphoreType.DMA
        vm = pl.BlockSpec(memory_space=pltpu.VMEM)
        hbm = pl.BlockSpec(memory_space=pl.ANY)
        hidden, reward, policy = pl.pallas_call(
            functools.partial(kernel, n, R, kvw, heads),
            out_shape=(
                jax.ShapeDtypeStruct(residual_in.shape, BF16),
                jax.ShapeDtypeStruct((8, 128), F32),
                jax.ShapeDtypeStruct(policy_slots.shape, BF16),
            ),
            in_specs=[hbm, vm, hbm, hbm, hbm, vm, pl.BlockSpec(memory_space=pltpu.SMEM), hbm],
            out_specs=(hbm, vm, hbm),
            scratch_shapes=[
                pltpu.VMEM((C, cols, qw), BF16),
                pltpu.VMEM((C, cols, kvw), BF16),
                pltpu.VMEM((C, qw, cols), BF16),
                pltpu.VMEM((C, rows, cols), BF16),
                pltpu.VMEM((n, C, rows, cols), BF16),
                pltpu.VMEM((n + 1, C, rows, cols), BF16),
                pltpu.VMEM((n, rows, qw), F32),
                pltpu.VMEM((n, rows, kvw), F32),
                pltpu.VMEM((n, kvw // HS, rows, HS), BF16),
                pltpu.VMEM((n, 2, rows, HS), BF16),
                pltpu.VMEM((n * rows, HS), BF16),
                pltpu.VMEM((n * rows, HS), BF16),
                pltpu.VMEM((n, rows, qw), BF16),
                pltpu.VMEM((rows, 128), F32),
                pltpu.VMEM((8, 128), F32),
                pltpu.VMEM((n - 1, 8, 128), F32),
                sem((2 * C + 2,)),
                sem((2, DEPTH)),
                sem((n, C)),
                sem((2, DEPTH)),
                sem((n + 1, C)),
                sem((n, kvw // HS, n - 1)),
                sem((n, 2)),
                sem((n - 1,)),
                sem((n - 1,)),
                sem((R.bit_length() - 1,)),
                sem,
                sem,
                sem((C,)),
                pltpu.SemaphoreType.REGULAR,
            ],
            compiler_params=pltpu.CompilerParams(
                collective_id=0, has_side_effects=True, vmem_limit_bytes=67043328
            ),
        )(
            residual_in,
            norm_gain.reshape(C, 1, cols),
            w_query.reshape(C, cols, qw),
            w_keyval.reshape(C, cols, kvw),
            w_out,
            score_head.reshape(C, 1, cols),
            lengths,
            policy_slots,
        )
        return hidden, reward[0, :1], policy

    return jax.shard_map(
        on_device,
        mesh=mesh,
        in_specs=(
            P("rep", "tp", None),
            P(),
            P(None, "tp"),
            P(None, "tp"),
            P("tp", None),
            P(),
            P("rep"),
            P("rep", None, "tp"),
        ),
        out_specs=(P("rep", "tp", None), P("rep"), P("rep", None, "tp")),
        check_vma=False,
    )
```

time: 301 us -> 238 us (0.79)
  Pallas kernels: 291 us -> 227 us
    pallas_call x1, Pallas kernels: 291 us -> 227 us  [on_device(): pl.pallas_call(functools.partial(kernel, n, R, kvw, heads), out_shape=(ja...]
where the time goes in v1:
time: 238 us; the launch traced here: 237 us
  Pallas kernels  227 us (95%)
  local copies, waits for them, and re-layouts  8.78 us (4%)
    pallas_call x1, Pallas kernels, on_device(): pl.pallas_call(functools.partial(kernel, n, R, kvw, heads), out_shape=(ja...  227 us
    unnamed x4, local copies, waits for them, and re-layouts  4.76 us

profile of v1, /device:TPU:1, one launch (start us, length us, event | category | flops | bytes accessed | tf_op | source)
XLA Modules:
  0.0 236.7 jit_solution(5755508819404419758)
XLA Ops:
  1.3 1.3 reshape.22.gain
  2.6 1.3 reshape.23.head
  4.0 226.6 %shard_map.103 = (bf16[1,128,8192]{2,1,0:T(8,128)(2,1)}, f32[8,128]{1,0:T(8,128)}, bf16[1,768,2048]{2,1,0:T(8,128)(2,1)}) custom-call(bf16[1,128,8192]{2,1,0:T(8,128)(2,1)} %resid_h.1, bf16[8,1,1024]{2,1,0:T(2,128)(2,1)} %reshape.22.gain, bf16[8,1024,1024]{2,1,0:T(8,128)(2,1)} %bitcast.3, bf16[8,1024,256]{2,1,0:T(8,128)(2,1)} %bitcast.4, ...), custom_call_target="tpu_custom_call" | custom-call | tf_op jit(solution)/shard_map/pallas_call | solution.py:464
  230.6 0.0 copy-start
  230.6 1.3 slice.3
  231.9 3.1 %copy.16 = bf16[1,128,8192]{2,1,0:T(8,128)(2,1)} copy(bf16[1,128,8192]{2,1,0:T(8,128)(2,1)} %get-tuple-element.12) | data formatting | bytes 4194304
  235.0 0.0 copy-done
  235.0 1.7 copy.17
Async XLA Ops:
  230.6 4.4 %copy-start = (bf16[1,768,2048]{2,1,0:T(8,128)(2,1)S(1)}, bf16[1,768,2048]{2,1,0:T(8,128)(2,1)}, u32[]{:S(2)}) copy-start(bf16[1,768,2048]{2,1,0:T(8,128)(2,1)} %get-tuple-element.14) | copy-start | bytes 9437188

commit v2 on v1

v2 whole, which is shorter than its diff:
```python
import functools

import jax
import jax.numpy as jnp
from jax import lax
from jax.experimental import pallas as pl
from jax.experimental.pallas import tpu as pltpu
from jax.sharding import PartitionSpec as P

QH = 32
KVH = 4
HS = 128
MESH = pl.DeviceIdType.MESH
F32 = jnp.float32
BF16 = jnp.bfloat16
CHUNKS = 16
DEPTH = 2
LAG = 2
NEVER = 1 << 20
UP, DOWN, MM_UP, MM_DOWN, ATTEND, SUM_UP, SUM_DOWN, FIN, SPREAD, PAIR, POLICY = range(11)
NOTHING = 15
PER_WORD = 7
POLICY_OPS = 4

PREFIX = {(4, 16): [0, 1, 2, 0]}
TUNED = {(4, 16): {
    (0, 0): [2, 101, 1, 101, 3, 801, 101, 1, 101, 1, 101, 1, 101, 1, 101, 1, 901, 101, 1, 301, 101, 301, 1, 302, 101, 301, 1, 303, 1001, 1, 101, 401, 1, 101, 401, 101, 304, 101, 303, 102, 301, 401, 101, 401, 502, 101, 301, 101, 501, 101, 301, 501, 101, 501, 101, 301, 501, 101, 501, 101, 301, 501, 101, 501, 101, 301, 501, 101, 501, 101, 301, 501, 1001, 101, 501, 101, 301, 501, 101, 501, 101, 501, 301, 401, 101, 401, 101, 502, 301, 101, 501, 101, 301, 501, 101, 501, 101, 301, 501, 101, 501, 101, 301, 501, 101, 501, 101, 301, 501, 101, 501, 101, 301, 501, 101, 501, 101, 301, 501, 101, 501, 101, 501, 1001, 301, 402, 502, 703, 501, 701, 501, 701, 501, 701, 501, 701, 501, 1001, 701, 501, 701, 501, 701, 501, 701, 501, 701, 501, 701, 501, 701, 501, 701, 501, 701, 501],
    (0, 1): [2, 101, 1, 101, 3, 801, 101, 1, 101, 1, 101, 1, 101, 1, 101, 1, 901, 101, 1, 301, 101, 301, 1, 302, 101, 301, 1, 303, 1001, 1, 101, 401, 1, 101, 401, 101, 304, 101, 303, 102, 301, 401, 101, 401, 502, 101, 301, 501, 101, 501, 101, 301, 501, 101, 501, 101, 301, 501, 101, 501, 101, 301, 501, 101, 501, 101, 301, 501, 101, 501, 101, 301, 1001, 501, 101, 501, 101, 301, 501, 101, 501, 101, 301, 401, 101, 401, 502, 101, 301, 501, 101, 502, 101, 301, 501, 101, 501, 101, 301, 501, 101, 501, 101, 301, 501, 101, 501, 101, 301, 501, 101, 501, 101, 301, 501, 101, 501, 101, 301, 501, 102, 1001, 301, 402, 502, 702, 501, 701, 501, 701, 501, 701, 501, 701, 501, 701, 1001, 501, 701, 501, 701, 501, 701, 501, 701, 501, 701, 501, 701, 501, 701, 501, 701, 501, 701],
    (1, 0): [1, 104, 2, 801, 101, 1, 101, 1, 101, 1, 101, 1, 101, 1, 101, 1, 101, 1, 101, 1, 101, 1, 901, 101, 1, 101, 1, 206, 1001, 1, 201, 1, 102, 302, 1, 201, 101, 401, 1, 401, 1, 101, 301, 101, 302, 1, 302, 101, 301, 1, 401, 101, 401, 1, 101, 301, 1, 301, 101, 302, 1, 101, 1, 101, 301, 1, 101, 1, 101, 301, 1, 101, 1, 101, 301, 1, 101, 1, 101, 1001, 301, 401, 1, 101, 401, 101, 301, 102, 301, 102, 301, 101, 501, 101, 501, 301, 101, 501, 101, 501, 301, 101, 501, 101, 501, 301, 101, 501, 101, 501, 301, 101, 501, 101, 501, 301, 401, 501, 601, 401, 501, 602, 502, 601, 701, 501, 601, 501, 701, 601, 701, 501, 1001, 601, 701, 501, 601, 701, 501, 601, 701, 501, 601, 701, 501, 601, 701, 501, 601, 701, 501, 601, 1001, 701, 501, 601, 701, 501, 601, 701, 501, 601, 701, 501, 701, 501, 701, 501, 701, 503],
    (1, 1): [1, 104, 2, 801, 101, 1, 101, 1, 101, 1, 101, 1, 101, 1, 101, 1, 101, 1, 101, 1, 101, 1, 901, 101, 1, 101, 1, 202, 1, 101, 202, 1001, 202, 1, 101, 201, 101, 301, 1, 201, 101, 401, 1, 401, 1, 101, 301, 101, 302, 1, 302, 101, 301, 1, 301, 101, 401, 1, 401, 1, 101, 302, 101, 301, 1, 301, 101, 301, 1, 101, 1, 101, 301, 1, 101, 1, 101, 301, 1, 101, 1, 101, 301, 1001, 1, 401, 101, 401, 1, 101, 301, 102, 301, 102, 301, 502, 101, 501, 101, 301, 501, 101, 501, 101, 301, 501, 101, 501, 101, 301, 501, 101, 501, 101, 301, 501, 101, 501, 101, 301, 401, 501, 601, 401, 501, 601, 501, 601, 501, 601, 501, 601, 701, 601, 501, 701, 501, 1001, 601, 701, 501, 601, 701, 501, 601, 701, 501, 601, 701, 501, 601, 701, 501, 601, 701, 501, 601, 1001, 701, 501, 601, 701, 501, 601, 701, 501, 601, 701, 501, 701, 501, 701, 501, 701, 501, 701, 501],
    (2, 0): [2, 103, 801, 101, 1, 101, 1, 101, 1, 101, 1, 101, 1, 101, 1, 101, 1, 101, 1, 101, 901, 1, 101, 1, 101, 202, 1, 101, 203, 1, 101, 1001, 201, 302, 1, 301, 101, 303, 1, 101, 201, 302, 1, 101, 301, 101, 301, 2, 201, 401, 1, 101, 401, 1, 101, 201, 301, 101, 1, 201, 101, 301, 1, 101, 1, 201, 101, 301, 1, 101, 1, 201, 101, 301, 1, 101, 1, 201, 101, 301, 1, 101, 1001, 1, 201, 101, 301, 1, 601, 1, 201, 601, 1, 601, 1, 201, 401, 1, 601, 401, 1, 601, 401, 1, 601, 401, 1, 601, 401, 601, 1, 401, 601, 1, 601, 1, 601, 1, 601, 1, 601, 1, 601, 1, 601, 1, 601, 1, 601, 1, 607, 501, 601, 1001, 501, 601, 701, 501, 601, 701, 501, 601, 701, 501, 601, 701, 501, 601, 701, 501, 601, 701, 501, 1001, 601, 701, 501, 701, 501, 701, 501, 701, 501, 701, 501, 701, 502, 701, 501, 703],
    (2, 1): [2, 103, 801, 101, 1, 101, 1, 101, 1, 101, 1, 101, 1, 101, 1, 101, 1, 101, 1, 101, 901, 1, 101, 1, 101, 202, 1, 101, 203, 1, 101, 1001, 201, 302, 1, 301, 101, 302, 1, 201, 101, 302, 1, 301, 101, 301, 1, 201, 101, 1, 401, 1, 401, 101, 1, 201, 101, 302, 1, 201, 101, 1, 101, 301, 1, 201, 101, 1, 101, 301, 1, 201, 101, 1, 101, 301, 1, 201, 101, 1, 101, 301, 1, 1001, 201, 101, 1, 101, 301, 1, 201, 601, 1, 601, 1, 201, 601, 401, 1, 601, 401, 1, 601, 401, 1, 401, 1, 601, 401, 601, 1, 401, 601, 1, 601, 1, 601, 1, 601, 1, 601, 1, 601, 1, 601, 1, 601, 1, 601, 1, 606, 501, 601, 501, 601, 1001, 501, 701, 601, 501, 701, 601, 501, 701, 601, 501, 701, 601, 501, 701, 601, 501, 701, 601, 501, 1001, 701, 601, 501, 701, 601, 501, 701, 501, 701, 501, 701, 501, 701, 501, 701, 501, 703],
    (3, 0): [106, 801, 102, 1, 101, 1, 101, 1, 101, 901, 1, 101, 201, 1, 201, 101, 302, 1, 201, 101, 302, 1, 301, 101, 302, 1001, 301, 1, 101, 201, 2, 201, 2, 201, 2, 201, 2, 201, 401, 1, 401, 602, 1, 201, 1, 601, 1, 201, 601, 1, 601, 1, 201, 601, 1, 601, 1, 201, 601, 1, 601, 1, 201, 601, 1, 601, 1, 201, 601, 1, 601, 1001, 1, 201, 601, 1, 601, 3, 601, 201, 401, 1, 401, 602, 1, 202, 1, 601, 1, 201, 601, 1, 601, 1, 201, 601, 1, 601, 1, 201, 601, 1, 601, 1, 201, 601, 1, 601, 1, 201, 601, 1, 601, 1, 201, 401, 601, 401, 601, 1001, 401, 601, 401, 603, 701, 601, 701, 602, 701, 601, 701, 601, 701, 601, 1001, 701, 601, 701, 601, 701, 601, 701, 601, 701, 601, 701, 601, 701, 601, 704],
    (3, 1): [106, 801, 102, 1, 101, 1, 101, 1, 101, 901, 1, 101, 301, 1, 301, 101, 302, 1, 301, 101, 302, 1, 301, 101, 202, 1001, 1, 201, 101, 201, 2, 201, 2, 201, 2, 201, 2, 201, 401, 1, 401, 601, 1, 601, 201, 601, 1, 601, 1, 201, 601, 1, 601, 1, 201, 601, 1, 601, 1, 201, 601, 1, 601, 1, 201, 601, 1, 601, 1, 201, 601, 1, 1001, 601, 1, 201, 601, 1, 601, 3, 201, 401, 1, 401, 1, 602, 202, 1, 602, 1, 201, 601, 1, 601, 1, 201, 601, 1, 601, 1, 201, 601, 1, 601, 1, 201, 601, 1, 601, 1, 201, 601, 1, 601, 1, 201, 401, 601, 401, 1001, 601, 401, 601, 401, 602, 701, 601, 701, 601, 701, 601, 701, 601, 701, 601, 701, 1001, 601, 701, 601, 701, 601, 701, 601, 701, 601, 701, 601, 701, 601, 701, 601, 703],
}}
TUNED = {size: {key: [run // 100 for run in runs for _ in range(run % 100)] for key, runs in found.items()} for size, found in TUNED.items()}


def plan(n, C):
    if (n, C) in TUNED:
        return TUNED[n, C], PREFIX[n, C]
    table = {}
    for t in range(n):
        w = n - 1 - t
        ops = [(-2, SPREAD), (-1, PAIR)]
        up = {(b, c): b * C + c + LAG * t for b in range(min(t + 1, n - 1)) for c in range(C)}
        down = {(b, c): (b - t) * C + c + LAG * w for b in range(max(t, 1), n) for c in range(C)}
        ops += [(k, UP) for k in up.values()] + [(k, DOWN) for k in down.values()]
        base = n * C + LAG * n
        ops += [(base, MM_UP)] * (t * C // 2) + [(base, MM_DOWN)] * ((n - t) * C // 2)
        ops += [(base, ATTEND)] * (2 * n)
        ops += [(base + 1 + (b - 1) * C + c + 2 * t, SUM_UP) for b in range(t + 1, n) for c in range(C)]
        ops += [(base + 1 + b * C + c + 2 * w, SUM_DOWN) for b in range(t) for c in range(C)]
        ops += [(base + n * C + 2 * n, FIN)] * C
        order = [op for _, op in sorted(ops)]
        for i in range(POLICY_OPS):
            order.insert(len(order) * (i + 1) // (POLICY_OPS + 1), POLICY)
        table[t, 0] = table[t, 1] = order
    return table, [0] * n


def kernel(
    n, R, kvw, heads,
    resid_h, gain, wq_h, wkv_h, wo_h, head, lens, pol_in,
    out_h, rew, pol_out,
    wq, wkv, wo, resid, nrm, part, accq, acckv, kf, vf, att, score, rmy, rin,
    load_sem, send_sem, ag_recv, rs_recv, w_load, w_send, w_recv, r_send, r_recv, p_send, p_recv, p_loc, out_sem,
):
    t = lax.axis_index("tp")
    r = lax.axis_index("rep")
    par = lax.rem(r, 2)
    C = nrm.shape[1]
    rows, cols = nrm.shape[2], nrm.shape[3]
    seq = n * rows
    length = lens[0]
    qw = att.shape[2]

    def chunk_of(ref, c):
        return ref.at[:, pl.ds(pl.multiple_of(c * cols, cols), cols)]

    loads = [pltpu.make_async_copy(chunk_of(resid_h.at[0], c), resid.at[c], load_sem.at[c]) for c in range(C)]
    wload = pltpu.make_async_copy(wq_h, wq, load_sem.at[C])
    oloads = [pltpu.make_async_copy(chunk_of(wo_h, c), wo.at[c], load_sem.at[C + 2 + c]) for c in range(C)]
    for cp in loads:
        cp.start()

    barrier = pltpu.get_barrier_semaphore()
    for k in range(1, n):
        pl.semaphore_signal(barrier, inc=1, device_id={"tp": lax.rem(t + k, n)}, device_id_type=MESH)
    for k in range(1, R):
        pl.semaphore_signal(barrier, inc=1, device_id={"rep": lax.rem(r + k, R)}, device_id_type=MESH)

    pieces = kvw // HS
    group = QH // KVH
    wrows = wkv.shape[0] // R

    def head_of(tp):
        return (tp * heads) // group

    def source(is_v, tp):
        gid = is_v * KVH + head_of(tp)
        return gid // pieces, lax.rem(gid, pieces)

    def wpart(ref, part, col):
        return ref.at[pl.ds(pl.multiple_of(part * wrows, wrows), wrows), pl.ds(pl.multiple_of(col * HS, HS), HS)]

    def w_own(is_v):
        _, p = source(is_v, t)
        return pltpu.make_async_copy(
            wkv_h.at[:, pl.ds(pl.multiple_of(p * HS, HS), HS)], wkv.at[:, is_v * HS : (is_v + 1) * HS], w_load.at[is_v]
        )

    def w_give(is_v, k):
        target = lax.rem(t + k, n)
        owner, p = source(is_v, target)
        return owner == t, pltpu.make_async_remote_copy(
            wpart(wkv_h, r, p), wpart(wkv, r, is_v), w_send.at[0, is_v, k - 1], w_recv.at[is_v, r],
            device_id={"tp": target}, device_id_type=MESH,
        )

    def w_spread(is_v, k):
        return pltpu.make_async_remote_copy(
            wpart(wkv, r, is_v), wpart(wkv, r, is_v), w_send.at[1, is_v, k - 1], w_recv.at[is_v, r],
            device_id={"rep": lax.rem(r + 2 * k, R)}, device_id_type=MESH,
        )

    def w_pair(is_v, k):
        part = lax.rem(r + 2 * k, R)
        return pltpu.make_async_remote_copy(
            wpart(wkv, part, is_v), wpart(wkv, part, is_v), w_send.at[2, is_v, k], w_recv.at[is_v, part],
            device_id={"rep": r + 1 - 2 * par}, device_id_type=MESH,
        )

    def w_wait(is_v, part):
        pltpu.make_async_copy(wpart(wkv, part, is_v), wpart(wkv, part, is_v), w_recv.at[is_v, part]).wait()

    def foreign(is_v, do):
        owner, _ = source(is_v, t)

        @pl.when(owner != t)
        def _():
            do()

    def spread():
        for is_v in (0, 1):
            def do(is_v=is_v):
                w_wait(is_v, r)
                for k in range(1, R // 2):
                    w_spread(is_v, k).start()
            foreign(is_v, do)

    def pair():
        for is_v in (0, 1):
            def do(is_v=is_v):
                w_pair(is_v, 0).start()
                for k in range(1, R // 2):
                    w_wait(is_v, lax.rem(r + 2 * k, R))
                    w_pair(is_v, k).start()
            foreign(is_v, do)

    def weights_here():
        wload.wait()
        for is_v in (0, 1):
            owner, _ = source(is_v, t)

            @pl.when(owner == t)
            def _(is_v=is_v):
                w_own(is_v).wait()

            def do(is_v=is_v):
                for k in range(R // 2):
                    w_wait(is_v, lax.rem(r + 1 - 2 * par + 2 * k, R))
            foreign(is_v, do)

    def weights_drain():
        for is_v in (0, 1):
            for k in range(1, n):
                mine, cp = w_give(is_v, k)

                @pl.when(mine)
                def _(cp=cp):
                    cp.wait_send()

            def do(is_v=is_v):
                for k in range(1, R // 2):
                    w_spread(is_v, k).wait_send()
                for k in range(R // 2):
                    w_pair(is_v, k).wait_send()
            foreign(is_v, do)

    kf[...] = jnp.zeros_like(kf)
    vf[...] = jnp.zeros_like(vf)
    score[...] = jnp.zeros_like(score)
    for b in range(n):
        accq[b] = jnp.zeros(accq.shape[1:], F32)
        acckv[b] = jnp.zeros(acckv.shape[1:], F32)

    pl.semaphore_wait(barrier, n - 1 + R - 1)
    for is_v in (0, 1):
        for k in range(1, n):
            mine, cp = w_give(is_v, k)

            @pl.when(mine)
            def _(cp=cp):
                cp.start()

    for cp in loads:
        cp.wait()
    for is_v in (0, 1):
        owner, _ = source(is_v, t)

        @pl.when(owner == t)
        def _(is_v=is_v):
            w_own(is_v).start()

    for cp in [wload] + oloads:
        cp.start()

    def sq(c, acc):
        x = resid[c].astype(F32)
        return acc + jnp.sum(x * x, axis=1, keepdims=True)

    ms = lax.fori_loop(0, C, sq, jnp.zeros((rows, 1), F32))
    scale = lax.rsqrt(ms / (C * cols) + 1e-05)

    def norm(c, carry):
        nrm[t, c] = (resid[c].astype(F32) * scale * gain[c].astype(F32)).astype(BF16)
        return carry

    lax.fori_loop(0, C, norm, 0)

    steps = R.bit_length() - 1

    def pol(src, s):
        return pltpu.make_async_remote_copy(
            src, pol_out, p_send.at[s], p_recv, device_id={"rep": r + (R >> (s + 1))}, device_id_type=MESH
        )

    def pol_root():
        @pl.when(r == 0)
        def _():
            for s in range(steps):
                pol(pol_in, s).start()
            pltpu.make_async_copy(pol_in, pol_out, p_loc).start()

    def pol_point(s):
        gap = R >> (s + 1)

        @pl.when(lax.rem(r, 2 * gap) == gap)
        def _():
            pltpu.make_async_copy(pol_out, pol_out, p_recv).wait()
            for q in range(s + 1, steps):
                pol(pol_out, q).start()

    table, prefix = plan(n, C)
    total_ops = max(len(ops) for ops in table.values())
    word_count = -(-total_ops // PER_WORD)

    def packed(ops, i):
        part = (ops + [NOTHING] * (word_count * PER_WORD))[i * PER_WORD : (i + 1) * PER_WORD]
        return sum(op << (4 * q) for q, op in enumerate(part))

    def pick(value):
        keys = list(table)
        out = jnp.int32(value(keys[0]))
        for a, p in keys[1:]:
            out = jnp.where((t == a) & (par == p), jnp.int32(value((a, p))), out)
        return out

    words = [pick(lambda key, i=i: packed(table[key], i)) for i in range(word_count)]
    ahead = pick(lambda key: prefix[key[0]])

    def multiply(b, q):
        x0, x1 = nrm[b, 2 * q], nrm[b, 2 * q + 1]
        w0 = wkv[pl.ds(pl.multiple_of(2 * q * cols, cols), cols), :]
        w1 = wkv[pl.ds(pl.multiple_of((2 * q + 1) * cols, cols), cols), :]
        acckv[b] += jnp.dot(x0, w0, preferred_element_type=F32) + jnp.dot(x1, w1, preferred_element_type=F32)
        accq[b] += jnp.dot(x0, wq[2 * q], preferred_element_type=F32) + jnp.dot(
            x1, wq[2 * q + 1], preferred_element_type=F32
        )

        @pl.when(q == C // 2 - 1)
        def _():
            span = pl.ds(pl.multiple_of(b * rows, rows), rows)
            kf[span, :] = acckv[b, :, :HS].astype(BF16)
            vf[span, :] = acckv[b, :, HS:].astype(BF16)

    def ag_copy(d, b, c, slot):
        return pltpu.make_async_remote_copy(
            nrm.at[b, c], nrm.at[b, c], send_sem.at[d, slot], ag_recv.at[b, c],
            device_id={"tp": t + (1 if d == 0 else -1)}, device_id_type=MESH,
        )

    def ag_step(d, i, sent):
        has = (t < n - 1) if d == 0 else (t > 0)
        if d == 0:
            edge = jnp.where(t == n - 1, 0, ahead)
            low = i - edge
            passing = (low >= 0) & (low < t * C)
            own_c = jnp.where(low < 0, i, i - t * C)
            b = jnp.where(passing, jnp.maximum(low, 0) // C, t)
            c = jnp.where(passing, lax.rem(jnp.maximum(low, 0), C), own_c)
        else:
            b = jnp.maximum(t, 1) + i // C
            c = lax.rem(i, C)

        @pl.when(b != t)
        def _():
            pltpu.make_async_copy(nrm.at[b, c], nrm.at[b, c], ag_recv.at[b, c]).wait()

        @pl.when(has)
        def _():
            @pl.when(sent >= DEPTH)
            def _():
                ag_copy(d, b, c, lax.rem(sent, DEPTH)).wait_send()

            ag_copy(d, b, c, lax.rem(sent, DEPTH)).start()

    def rs_copy(d, b, c, slot):
        dst = b if d == 0 else jnp.where(b == t - 1, n, b)
        return pltpu.make_async_remote_copy(
            part.at[b, c], part.at[dst, c], send_sem.at[d, slot], rs_recv.at[dst, c],
            device_id={"tp": t + (1 if d == 0 else -1)}, device_id_type=MESH,
        )

    def rs_wait(slot, c):
        pltpu.make_async_copy(part.at[slot, c], part.at[slot, c], rs_recv.at[slot, c]).wait()

    def project(b, c):
        return jnp.dot(att[b], wo[c], preferred_element_type=F32).astype(BF16)

    def rs_step(d, i, sent):
        b = (t + 1 if d == 0 else 0) + i // C
        c = lax.rem(i, C)
        has = (t > 0) if d == 0 else (t < n - 1)
        mine = project(b, c)

        @pl.when(has)
        def _():
            rs_wait(b, c)
            part[b, c] = (part[b, c].astype(F32) + mine.astype(F32)).astype(BF16)

        @pl.when(jnp.logical_not(has))
        def _():
            part[b, c] = mine

        @pl.when(sent >= DEPTH)
        def _():
            rs_copy(d, b, c, lax.rem(sent, DEPTH)).wait_send()

        rs_copy(d, b, c, lax.rem(sent, DEPTH)).start()

    def attend(b, part_of):
        rowpos = b * rows + lax.broadcasted_iota(jnp.int32, (rows, seq), 0)
        colpos = lax.broadcasted_iota(jnp.int32, (rows, seq), 1)
        valid = (colpos <= rowpos) & (colpos < length)
        wide = qw // 2
        here = pl.ds(pl.multiple_of(part_of * wide, wide), wide)
        q = accq[b, :, here].astype(BF16)
        outs = []
        for h in range(heads // 2):
            s = lax.dot_general(
                q[:, h * HS : (h + 1) * HS], kf[...],
                (((1,), (1,)), ((), ())), preferred_element_type=F32,
            ) * HS ** (-0.5)
            s = jnp.where(valid, s, -1e30)
            e = jnp.exp(s - jnp.max(s, axis=1, keepdims=True))
            pr = (e / jnp.sum(e, axis=1, keepdims=True)).astype(BF16)
            outs.append(jnp.dot(pr, vf[...], preferred_element_type=F32).astype(BF16))
        att[b, :, here] = jnp.concatenate(outs, axis=1)

    def fin(c):
        total = project(t, c).astype(F32)

        @pl.when(t > 0)
        def _():
            rs_wait(t, c)

        @pl.when(t < n - 1)
        def _():
            rs_wait(n, c)

        below = jnp.where(t > 0, part[t, c].astype(F32), 0.0)
        above = jnp.where(t < n - 1, part[n, c].astype(F32), 0.0)
        hid = (resid[c].astype(F32) + (total + below + above)).astype(BF16)
        resid[c] = hid
        pltpu.make_async_copy(resid.at[c], chunk_of(out_h.at[0], c), out_sem.at[c]).start()
        weighed = hid.astype(F32) * head[c].astype(F32)
        acc = score[...]
        for q in range(cols // HS):
            acc = acc + weighed[:, q * HS : (q + 1) * HS]
        score[...] = acc


    def policy(i):
        @pl.when(i == 0)
        def _():
            pol_root()

        for s in range(steps - 1):
            @pl.when(i == min(s + 1, POLICY_OPS - 1))
            def _(s=s):
                pol_point(s)

    def one(k, pos):
        word = words[0]
        for i in range(1, word_count):
            word = jnp.where(k // PER_WORD == i, words[i], word)
        op = lax.rem(lax.shift_right_logical(word, 4 * lax.rem(k, PER_WORD)), 16)

        def at(kind, do):
            @pl.when(op == kind)
            def _():
                do(pos[kind])

        half = C // 2
        at(UP, lambda i: ag_step(0, i, i + pos[SUM_UP]))
        at(DOWN, lambda i: ag_step(1, i, i + pos[SUM_DOWN]))

        @pl.when((op == MM_UP) | (op == MM_DOWN))
        def _():
            first = pos[MM_UP] + pos[MM_DOWN] == 0

            @pl.when(first)
            def _():
                weights_here()

            i = jnp.where(op == MM_UP, pos[MM_UP], pos[MM_DOWN] + t * half)
            multiply(i // half, lax.rem(i, half))

        at(ATTEND, lambda i: attend(i // 2, lax.rem(i, 2)))

        @pl.when((op == SUM_UP) | (op == SUM_DOWN) | (op == FIN))
        def _():
            @pl.when(pos[SUM_UP] + pos[SUM_DOWN] + pos[FIN] == 0)
            def _():
                for cp in oloads:
                    cp.wait()

        at(SUM_UP, lambda i: rs_step(0, i, i + pos[UP]))
        at(SUM_DOWN, lambda i: rs_step(1, i, i + pos[DOWN]))
        at(FIN, fin)
        at(SPREAD, lambda i: spread())
        at(PAIR, lambda i: pair())
        at(POLICY, policy)
        return tuple(p + jnp.where(op == kind, 1, 0) for kind, p in enumerate(pos))

    lax.fori_loop(0, total_ops, one, (jnp.int32(0),) * 11)

    local_last = length - 1 - t * rows
    rowid = lax.broadcasted_iota(jnp.int32, (rows, 1), 0)
    weight = jnp.where(rowid == local_last, 1.0, 0.0) + seq ** (-0.5)
    rmy[...] = jnp.broadcast_to(jnp.sum(score[...] * weight, keepdims=True), rmy.shape)

    def rcopy(k):
        return pltpu.make_async_remote_copy(
            rmy, rin.at[k - 1], r_send.at[k - 1], r_recv.at[k - 1],
            device_id={"tp": lax.rem(t + k, n)}, device_id_type=MESH,
        )

    for k in range(1, n):
        rcopy(k).start()
    pol_point(steps - 1)

    for d in (0, 1):
        has = (t < n - 1) if d == 0 else (t > 0)

        @pl.when(has)
        def _(d=d):
            for q in range(DEPTH):
                ag_copy(d, t, 0, q).wait_send()

    weights_drain()

    total = rmy[...]
    for k in range(1, n):
        rcopy(k).wait()
        total = total + rin[k - 1]
    rew[...] = total
    for c in range(C):
        pltpu.make_async_copy(resid.at[c], chunk_of(out_h.at[0], c), out_sem.at[c]).wait()

    @pl.when(r == 0)
    def _():
        for s in range(steps):
            pol(pol_in, s).wait_send()
        pltpu.make_async_copy(pol_in, pol_out, p_loc).wait()

    for s in range(steps - 1):
        gap = R >> (s + 1)

        @pl.when(lax.rem(r, 2 * gap) == gap)
        def _(s=s):
            for q in range(s + 1, steps):
                pol(pol_out, q).wait_send()


def solution(mesh):
    n, R = mesh.shape["tp"], mesh.shape["rep"]

    def on_device(residual_in, norm_gain, w_query, w_keyval, w_out, score_head, lengths, policy_slots):
        rows, width = residual_in.shape[1:]
        qw, kvw = w_query.shape[1], w_keyval.shape[1]
        heads = qw // HS
        C = CHUNKS
        cols = width // C
        sem = pltpu.SemaphoreType.DMA
        vm = pl.BlockSpec(memory_space=pltpu.VMEM)
        hbm = pl.BlockSpec(memory_space=pl.ANY)
        hidden, reward, policy = pl.pallas_call(
            functools.partial(kernel, n, R, kvw, heads),
            out_shape=(
                jax.ShapeDtypeStruct(residual_in.shape, BF16),
                jax.ShapeDtypeStruct((8, 128), F32),
                jax.ShapeDtypeStruct(policy_slots.shape, BF16),
            ),
            in_specs=[hbm, vm, hbm, hbm, hbm, vm, pl.BlockSpec(memory_space=pltpu.SMEM), hbm],
            out_specs=(hbm, vm, hbm),
            scratch_shapes=[
                pltpu.VMEM((C, cols, qw), BF16),
                pltpu.VMEM((width, 2 * HS), BF16),
                pltpu.VMEM((C, qw, cols), BF16),
                pltpu.VMEM((C, rows, cols), BF16),
                pltpu.VMEM((n, C, rows, cols), BF16),
                pltpu.VMEM((n + 1, C, rows, cols), BF16),
                pltpu.VMEM((n, rows, qw), F32),
                pltpu.VMEM((n, rows, 2 * HS), F32),
                pltpu.VMEM((n * rows, HS), BF16),
                pltpu.VMEM((n * rows, HS), BF16),
                pltpu.VMEM((n, rows, qw), BF16),
                pltpu.VMEM((rows, 128), F32),
                pltpu.VMEM((8, 128), F32),
                pltpu.VMEM((n - 1, 8, 128), F32),
                sem((2 * C + 2,)),
                sem((2, DEPTH)),
                sem((n, C)),
                sem((n + 1, C)),
                sem((2,)),
                sem((3, 2, max(n, R // 2))),
                sem((2, R)),
                sem((n - 1,)),
                sem((n - 1,)),
                sem((R.bit_length() - 1,)),
                sem,
                sem,
                sem((C,)),
            ],
            compiler_params=pltpu.CompilerParams(
                collective_id=0, has_side_effects=True, vmem_limit_bytes=67043328
            ),
        )(
            residual_in,
            norm_gain.reshape(C, 1, cols),
            w_query.reshape(C, cols, qw),
            w_keyval,
            w_out,
            score_head.reshape(C, 1, cols),
            lengths,
            policy_slots,
        )
        return hidden, reward[0, :1], policy

    return jax.shard_map(
        on_device,
        mesh=mesh,
        in_specs=(
            P("rep", "tp", None),
            P(),
            P(None, "tp"),
            P(None, "tp"),
            P("tp", None),
            P(),
            P("rep"),
            P("rep", None, "tp"),
        ),
        out_specs=(P("rep", "tp", None), P("rep"), P("rep", None, "tp")),
        check_vma=False,
    )
```

time: 238 us -> 234 us (0.983)
  the two profiles are of different devices: /device:TPU:1 before, /device:TPU:0 now
where the time goes in v2:
time: 234 us
  Pallas kernels  224 us (96%)
  local copies, waits for them, and re-layouts  8.78 us (4%)
    pallas_call x1, Pallas kernels, on_device(): pl.pallas_call(functools.partial(kernel, n, R, kvw, heads), out_shape=(ja...  224 us
    unnamed x4, local copies, waits for them, and re-layouts  4.76 us

profile of v2, /device:TPU:0, one launch (start us, length us, event | category | flops | bytes accessed | tf_op | source)
XLA Modules:
  0.0 234.1 jit_solution(418604014311241085)
XLA Ops:
  1.3 1.3 reshape.18.gain
  2.6 1.3 reshape.19.head
  4.0 224.0 %shard_map.103 = (bf16[1,128,8192]{2,1,0:T(8,128)(2,1)}, f32[8,128]{1,0:T(8,128)}, bf16[1,768,2048]{2,1,0:T(8,128)(2,1)}) custom-call(bf16[1,128,8192]{2,1,0:T(8,128)(2,1)} %resid_h.1, bf16[16,1,512]{2,1,0:T(2,128)(2,1)} %reshape.18.gain, bf16[16,512,1024]{2,1,0:T(8,128)(2,1)} %bitcast.2, bf16[8192,256]{1,0:T(8,128)(2,1)} %wkv_h.1, bf16[1024,8192]{1,0:T(8,128)(2,1)} %wo_h.1, ...), custom_call_target="tpu_custom_call" | custom-call | tf_op jit(solution)/shard_map/pallas_call | solution.py:510
  228.0 0.0 copy-start
  228.0 1.3 slice.3
  229.4 3.1 %copy.16 = bf16[1,128,8192]{2,1,0:T(8,128)(2,1)} copy(bf16[1,128,8192]{2,1,0:T(8,128)(2,1)} %get-tuple-element.12) | data formatting | bytes 4194304
  232.4 0.0 copy-done
  232.5 1.7 copy.17
Async XLA Ops:
  228.0 4.4 %copy-start = (bf16[1,768,2048]{2,1,0:T(8,128)(2,1)S(1)}, bf16[1,768,2048]{2,1,0:T(8,128)(2,1)}, u32[]{:S(2)}) copy-start(bf16[1,768,2048]{2,1,0:T(8,128)(2,1)} %get-tuple-element.14) | copy-start | bytes 9437188

commit v3 on v2

--- a/solution.py
+++ b/solution.py
@@ -13,7 +13,7 @@
 MESH = pl.DeviceIdType.MESH
 F32 = jnp.float32
 BF16 = jnp.bfloat16
-CHUNKS = 16
+CHUNKS = 8
 DEPTH = 2
 LAG = 2
 NEVER = 1 << 20
@@ -22,23 +22,24 @@
 PER_WORD = 7
 POLICY_OPS = 4
 
-PREFIX = {(4, 16): [0, 1, 2, 0]}
-TUNED = {(4, 16): {
-    (0, 0): [2, 101, 1, 101, 3, 801, 101, 1, 101, 1, 101, 1, 101, 1, 101, 1, 901, 101, 1, 301, 101, 301, 1, 302, 101, 301, 1, 303, 1001, 1, 101, 401, 1, 101, 401, 101, 304, 101, 303, 102, 301, 401, 101, 401, 502, 101, 301, 101, 501, 101, 301, 501, 101, 501, 101, 301, 501, 101, 501, 101, 301, 501, 101, 501, 101, 301, 501, 101, 501, 101, 301, 501, 1001, 101, 501, 101, 301, 501, 101, 501, 101, 501, 301, 401, 101, 401, 101, 502, 301, 101, 501, 101, 301, 501, 101, 501, 101, 301, 501, 101, 501, 101, 301, 501, 101, 501, 101, 301, 501, 101, 501, 101, 301, 501, 101, 501, 101, 301, 501, 101, 501, 101, 501, 1001, 301, 402, 502, 703, 501, 701, 501, 701, 501, 701, 501, 701, 501, 1001, 701, 501, 701, 501, 701, 501, 701, 501, 701, 501, 701, 501, 701, 501, 701, 501, 701, 501],
-    (0, 1): [2, 101, 1, 101, 3, 801, 101, 1, 101, 1, 101, 1, 101, 1, 101, 1, 901, 101, 1, 301, 101, 301, 1, 302, 101, 301, 1, 303, 1001, 1, 101, 401, 1, 101, 401, 101, 304, 101, 303, 102, 301, 401, 101, 401, 502, 101, 301, 501, 101, 501, 101, 301, 501, 101, 501, 101, 301, 501, 101, 501, 101, 301, 501, 101, 501, 101, 301, 501, 101, 501, 101, 301, 1001, 501, 101, 501, 101, 301, 501, 101, 501, 101, 301, 401, 101, 401, 502, 101, 301, 501, 101, 502, 101, 301, 501, 101, 501, 101, 301, 501, 101, 501, 101, 301, 501, 101, 501, 101, 301, 501, 101, 501, 101, 301, 501, 101, 501, 101, 301, 501, 102, 1001, 301, 402, 502, 702, 501, 701, 501, 701, 501, 701, 501, 701, 501, 701, 1001, 501, 701, 501, 701, 501, 701, 501, 701, 501, 701, 501, 701, 501, 701, 501, 701, 501, 701],
-    (1, 0): [1, 104, 2, 801, 101, 1, 101, 1, 101, 1, 101, 1, 101, 1, 101, 1, 101, 1, 101, 1, 101, 1, 901, 101, 1, 101, 1, 206, 1001, 1, 201, 1, 102, 302, 1, 201, 101, 401, 1, 401, 1, 101, 301, 101, 302, 1, 302, 101, 301, 1, 401, 101, 401, 1, 101, 301, 1, 301, 101, 302, 1, 101, 1, 101, 301, 1, 101, 1, 101, 301, 1, 101, 1, 101, 301, 1, 101, 1, 101, 1001, 301, 401, 1, 101, 401, 101, 301, 102, 301, 102, 301, 101, 501, 101, 501, 301, 101, 501, 101, 501, 301, 101, 501, 101, 501, 301, 101, 501, 101, 501, 301, 101, 501, 101, 501, 301, 401, 501, 601, 401, 501, 602, 502, 601, 701, 501, 601, 501, 701, 601, 701, 501, 1001, 601, 701, 501, 601, 701, 501, 601, 701, 501, 601, 701, 501, 601, 701, 501, 601, 701, 501, 601, 1001, 701, 501, 601, 701, 501, 601, 701, 501, 601, 701, 501, 701, 501, 701, 501, 701, 503],
-    (1, 1): [1, 104, 2, 801, 101, 1, 101, 1, 101, 1, 101, 1, 101, 1, 101, 1, 101, 1, 101, 1, 101, 1, 901, 101, 1, 101, 1, 202, 1, 101, 202, 1001, 202, 1, 101, 201, 101, 301, 1, 201, 101, 401, 1, 401, 1, 101, 301, 101, 302, 1, 302, 101, 301, 1, 301, 101, 401, 1, 401, 1, 101, 302, 101, 301, 1, 301, 101, 301, 1, 101, 1, 101, 301, 1, 101, 1, 101, 301, 1, 101, 1, 101, 301, 1001, 1, 401, 101, 401, 1, 101, 301, 102, 301, 102, 301, 502, 101, 501, 101, 301, 501, 101, 501, 101, 301, 501, 101, 501, 101, 301, 501, 101, 501, 101, 301, 501, 101, 501, 101, 301, 401, 501, 601, 401, 501, 601, 501, 601, 501, 601, 501, 601, 701, 601, 501, 701, 501, 1001, 601, 701, 501, 601, 701, 501, 601, 701, 501, 601, 701, 501, 601, 701, 501, 601, 701, 501, 601, 1001, 701, 501, 601, 701, 501, 601, 701, 501, 601, 701, 501, 701, 501, 701, 501, 701, 501, 701, 501],
-    (2, 0): [2, 103, 801, 101, 1, 101, 1, 101, 1, 101, 1, 101, 1, 101, 1, 101, 1, 101, 1, 101, 901, 1, 101, 1, 101, 202, 1, 101, 203, 1, 101, 1001, 201, 302, 1, 301, 101, 303, 1, 101, 201, 302, 1, 101, 301, 101, 301, 2, 201, 401, 1, 101, 401, 1, 101, 201, 301, 101, 1, 201, 101, 301, 1, 101, 1, 201, 101, 301, 1, 101, 1, 201, 101, 301, 1, 101, 1, 201, 101, 301, 1, 101, 1001, 1, 201, 101, 301, 1, 601, 1, 201, 601, 1, 601, 1, 201, 401, 1, 601, 401, 1, 601, 401, 1, 601, 401, 1, 601, 401, 601, 1, 401, 601, 1, 601, 1, 601, 1, 601, 1, 601, 1, 601, 1, 601, 1, 601, 1, 601, 1, 607, 501, 601, 1001, 501, 601, 701, 501, 601, 701, 501, 601, 701, 501, 601, 701, 501, 601, 701, 501, 601, 701, 501, 1001, 601, 701, 501, 701, 501, 701, 501, 701, 501, 701, 501, 701, 502, 701, 501, 703],
-    (2, 1): [2, 103, 801, 101, 1, 101, 1, 101, 1, 101, 1, 101, 1, 101, 1, 101, 1, 101, 1, 101, 901, 1, 101, 1, 101, 202, 1, 101, 203, 1, 101, 1001, 201, 302, 1, 301, 101, 302, 1, 201, 101, 302, 1, 301, 101, 301, 1, 201, 101, 1, 401, 1, 401, 101, 1, 201, 101, 302, 1, 201, 101, 1, 101, 301, 1, 201, 101, 1, 101, 301, 1, 201, 101, 1, 101, 301, 1, 201, 101, 1, 101, 301, 1, 1001, 201, 101, 1, 101, 301, 1, 201, 601, 1, 601, 1, 201, 601, 401, 1, 601, 401, 1, 601, 401, 1, 401, 1, 601, 401, 601, 1, 401, 601, 1, 601, 1, 601, 1, 601, 1, 601, 1, 601, 1, 601, 1, 601, 1, 601, 1, 606, 501, 601, 501, 601, 1001, 501, 701, 601, 501, 701, 601, 501, 701, 601, 501, 701, 601, 501, 701, 601, 501, 701, 601, 501, 1001, 701, 601, 501, 701, 601, 501, 701, 501, 701, 501, 701, 501, 701, 501, 701, 501, 703],
-    (3, 0): [106, 801, 102, 1, 101, 1, 101, 1, 101, 901, 1, 101, 201, 1, 201, 101, 302, 1, 201, 101, 302, 1, 301, 101, 302, 1001, 301, 1, 101, 201, 2, 201, 2, 201, 2, 201, 2, 201, 401, 1, 401, 602, 1, 201, 1, 601, 1, 201, 601, 1, 601, 1, 201, 601, 1, 601, 1, 201, 601, 1, 601, 1, 201, 601, 1, 601, 1, 201, 601, 1, 601, 1001, 1, 201, 601, 1, 601, 3, 601, 201, 401, 1, 401, 602, 1, 202, 1, 601, 1, 201, 601, 1, 601, 1, 201, 601, 1, 601, 1, 201, 601, 1, 601, 1, 201, 601, 1, 601, 1, 201, 601, 1, 601, 1, 201, 401, 601, 401, 601, 1001, 401, 601, 401, 603, 701, 601, 701, 602, 701, 601, 701, 601, 701, 601, 1001, 701, 601, 701, 601, 701, 601, 701, 601, 701, 601, 701, 601, 701, 601, 704],
-    (3, 1): [106, 801, 102, 1, 101, 1, 101, 1, 101, 901, 1, 101, 301, 1, 301, 101, 302, 1, 301, 101, 302, 1, 301, 101, 202, 1001, 1, 201, 101, 201, 2, 201, 2, 201, 2, 201, 2, 201, 401, 1, 401, 601, 1, 601, 201, 601, 1, 601, 1, 201, 601, 1, 601, 1, 201, 601, 1, 601, 1, 201, 601, 1, 601, 1, 201, 601, 1, 601, 1, 201, 601, 1, 1001, 601, 1, 201, 601, 1, 601, 3, 201, 401, 1, 401, 1, 602, 202, 1, 602, 1, 201, 601, 1, 601, 1, 201, 601, 1, 601, 1, 201, 601, 1, 601, 1, 201, 601, 1, 601, 1, 201, 601, 1, 601, 1, 201, 401, 601, 401, 1001, 601, 401, 601, 401, 602, 701, 601, 701, 601, 701, 601, 701, 601, 701, 601, 701, 1001, 601, 701, 601, 701, 601, 701, 601, 701, 601, 701, 601, 701, 601, 701, 601, 703],
+PREFIX = {(4, 8): [0, 0, 1, 0]}
+GATE = {(4, 8): ([7, 6, 6, 29], [29, 5, 16, 2])}
+TUNED = {(4, 8): {
+    (0, 0): [3, 101, 2, 101, 1, 801, 1, 101, 1, 102, 901, 303, 1001, 301, 402, 302, 101, 301, 102, 301, 402, 502, 102, 301, 501, 101, 501, 101, 501, 301, 501, 101, 501, 1001, 501, 101, 301, 102, 301, 402, 502, 102, 501, 301, 501, 101, 502, 101, 501, 301, 501, 102, 301, 102, 1001, 301, 402, 502, 702, 502, 1001, 701, 502, 701, 502, 704],
+    (0, 1): [801, 3, 101, 901, 1, 101, 1, 301, 101, 301, 1, 301, 1, 301, 101, 1, 1001, 302, 401, 101, 401, 101, 301, 102, 301, 402, 502, 102, 301, 502, 101, 501, 101, 301, 502, 101, 1001, 501, 101, 301, 102, 301, 402, 101, 502, 101, 301, 501, 101, 502, 101, 301, 502, 101, 501, 101, 301, 102, 1001, 301, 402, 502, 702, 501, 701, 1001, 502, 701, 502, 701, 501, 703],
+    (1, 0): [103, 1, 101, 1, 801, 1, 101, 2, 101, 1, 101, 1, 101, 2, 101, 1001, 901, 1, 101, 302, 1, 303, 1, 102, 301, 1, 202, 101, 201, 1, 201, 401, 1, 402, 1, 401, 101, 301, 101, 1001, 101, 301, 402, 102, 301, 102, 301, 501, 101, 502, 101, 301, 502, 101, 701, 501, 101, 501, 301, 401, 501, 401, 601, 701, 601, 1001, 702, 601, 701, 601, 701, 501, 601, 701, 1001, 501, 601, 501, 701, 501, 601, 502, 601, 502],
+    (1, 1): [801, 103, 1, 101, 1, 101, 1, 901, 101, 2, 301, 101, 303, 101, 1001, 202, 1, 201, 2, 201, 401, 101, 401, 101, 301, 402, 101, 2, 101, 301, 2, 101, 2, 101, 301, 2, 101, 1001, 101, 301, 402, 102, 301, 102, 301, 101, 501, 101, 301, 502, 101, 502, 101, 301, 502, 401, 601, 501, 401, 603, 1001, 601, 501, 701, 501, 601, 701, 501, 701, 501, 1001, 601, 701, 501, 701, 501, 601, 701, 501, 701, 501, 701],
+    (2, 0): [1, 103, 801, 1, 101, 1, 101, 1, 101, 1, 101, 1, 102, 1, 102, 1001, 1, 101, 901, 102, 1, 204, 1, 101, 401, 1, 201, 101, 401, 1, 302, 601, 1, 201, 601, 301, 1, 301, 601, 301, 1001, 301, 601, 1, 201, 1, 301, 601, 301, 1, 201, 601, 1, 402, 601, 1, 402, 601, 1, 402, 2, 601, 1, 601, 1, 602, 1001, 604, 703, 502, 1001, 701, 502, 701, 502, 701, 501, 701, 501, 701],
+    (2, 1): [801, 2, 901, 1, 201, 1, 303, 1, 201, 301, 1, 103, 1, 201, 1001, 101, 1, 101, 1, 201, 101, 402, 101, 2, 201, 101, 1, 101, 1, 201, 101, 301, 1, 101, 1, 201, 101, 301, 1, 101, 1, 201, 1001, 101, 402, 101, 402, 101, 2, 302, 402, 2, 602, 2, 601, 1, 609, 1001, 601, 501, 602, 501, 601, 501, 701, 501, 1001, 701, 501, 701, 501, 701, 501, 701, 501, 703],
+    (3, 0): [103, 801, 101, 1, 101, 2, 101, 901, 1, 202, 304, 1001, 2, 201, 1, 102, 1, 201, 402, 602, 1, 602, 1, 601, 201, 601, 1, 602, 1, 201, 2, 1001, 201, 2, 201, 402, 602, 2, 201, 1, 601, 1, 201, 601, 1, 601, 1, 201, 602, 1, 601, 1, 201, 401, 1001, 401, 602, 402, 604, 1001, 701, 601, 702, 601, 705],
+    (3, 1): [103, 801, 103, 901, 101, 304, 101, 2, 201, 1, 1001, 1, 201, 2, 201, 2, 201, 402, 602, 1, 601, 1, 601, 201, 601, 1, 602, 1, 201, 601, 2, 1001, 201, 2, 201, 402, 602, 2, 201, 1, 601, 1, 201, 1, 601, 1, 201, 1, 601, 1, 201, 401, 601, 402, 1001, 601, 401, 604, 701, 602, 1001, 701, 601, 701, 601, 701, 601, 704],
 }}
 TUNED = {size: {key: [run // 100 for run in runs for _ in range(run % 100)] for key, runs in found.items()} for size, found in TUNED.items()}
 
 
 def plan(n, C):
     if (n, C) in TUNED:
-        return TUNED[n, C], PREFIX[n, C]
+        return TUNED[n, C], PREFIX[n, C], GATE[n, C]
     table = {}
     for t in range(n):
         w = n - 1 - t
@@ -56,7 +57,7 @@
         for i in range(POLICY_OPS):
             order.insert(len(order) * (i + 1) // (POLICY_OPS + 1), POLICY)
         table[t, 0] = table[t, 1] = order
-    return table, [0] * n
+    return table, [0] * n, ([1] * n, [1] * n)
 
 
 def kernel(
@@ -64,7 +65,7 @@
     resid_h, gain, wq_h, wkv_h, wo_h, head, lens, pol_in,
     out_h, rew, pol_out,
     wq, wkv, wo, resid, nrm, part, accq, acckv, kf, vf, att, score, rmy, rin,
-    load_sem, send_sem, ag_recv, rs_recv, w_load, w_send, w_recv, r_send, r_recv, p_send, p_recv, p_loc, out_sem,
+    load_sem, send_sem, ag_recv, rs_recv, w_load, w_send, w_recv, r_send, r_recv, p_send, p_recv, p_loc, out_sem, go_sem,
 ):
     t = lax.axis_index("tp")
     r = lax.axis_index("rep")
@@ -252,7 +253,7 @@
             for q in range(s + 1, steps):
                 pol(pol_out, q).start()
 
-    table, prefix = plan(n, C)
+    table, prefix, gate = plan(n, C)
     total_ops = max(len(ops) for ops in table.values())
     word_count = -(-total_ops // PER_WORD)
 
@@ -269,6 +270,7 @@
 
     words = [pick(lambda key, i=i: packed(table[key], i)) for i in range(word_count)]
     ahead = pick(lambda key: prefix[key[0]])
+    release = [pick(lambda key, d=d: gate[d][key[0]]) for d in (0, 1)]
 
     def multiply(b, q):
         x0, x1 = nrm[b, 2 * q], nrm[b, 2 * q + 1]
@@ -308,6 +310,10 @@
         def _():
             pltpu.make_async_copy(nrm.at[b, c], nrm.at[b, c], ag_recv.at[b, c]).wait()
 
+        @pl.when(has & (par == 1) & (i == 0))
+        def _():
+            pl.semaphore_wait(go_sem.at[d], 1)
+
         @pl.when(has)
         def _():
             @pl.when(sent >= DEPTH)
@@ -315,6 +321,10 @@
                 ag_copy(d, b, c, lax.rem(sent, DEPTH)).wait_send()
 
             ag_copy(d, b, c, lax.rem(sent, DEPTH)).start()
+
+        @pl.when(has & (par == 0) & (i + 1 == release[d]))
+        def _():
+            pl.semaphore_signal(go_sem.at[d], inc=1, device_id={"rep": r + 1}, device_id_type=MESH)
 
     def rs_copy(d, b, c, slot):
         dst = b if d == 0 else jnp.where(b == t - 1, n, b)
@@ -544,6 +554,7 @@
                 sem,
                 sem,
                 sem((C,)),
+                pltpu.SemaphoreType.REGULAR((2,)),
             ],
             compiler_params=pltpu.CompilerParams(
                 collective_id=0, has_side_effects=True, vmem_limit_bytes=67043328

time: 234 us -> 233 us (level)
  the two profiles are of different devices: /device:TPU:0 before, /device:TPU:1 now
where the time goes in v3:
time: 233 us
  Pallas kernels  223 us (96%)
  local copies, waits for them, and re-layouts  8.78 us (4%)
    pallas_call x1, Pallas kernels, on_device(): pl.pallas_call(functools.partial(kernel, n, R, kvw, heads), out_shape=(ja...  223 us
    unnamed x4, local copies, waits for them, and re-layouts  4.76 us

profile of v3, /device:TPU:1, one launch (start us, length us, event | category | flops | bytes accessed | tf_op | source)
XLA Modules:
  0.0 232.6 jit_solution(14070685246391975070)
XLA Ops:
  1.3 1.3 reshape.18.gain
  2.6 1.3 reshape.19.head
  4.0 222.6 %shard_map.103 = (bf16[1,128,8192]{2,1,0:T(8,128)(2,1)}, f32[8,128]{1,0:T(8,128)}, bf16[1,768,2048]{2,1,0:T(8,128)(2,1)}) custom-call(bf16[1,128,8192]{2,1,0:T(8,128)(2,1)} %resid_h.1, bf16[8,1,1024]{2,1,0:T(2,128)(2,1)} %reshape.18.gain, bf16[8,1024,1024]{2,1,0:T(8,128)(2,1)} %bitcast.2, bf16[8192,256]{1,0:T(8,128)(2,1)} %wkv_h.1, bf16[1024,8192]{1,0:T(8,128)(2,1)} %wo_h.1, ...), custom_call_target="tpu_custom_call" | custom-call | tf_op jit(solution)/shard_map/pallas_call | solution.py:520
  226.5 0.0 copy-start
  226.5 1.3 slice.3
  227.9 3.1 %copy.16 = bf16[1,128,8192]{2,1,0:T(8,128)(2,1)} copy(bf16[1,128,8192]{2,1,0:T(8,128)(2,1)} %get-tuple-element.12) | data formatting | bytes 4194304
  231.0 0.0 copy-done
  231.0 1.7 copy.17
Async XLA Ops:
  226.5 4.4 %copy-start = (bf16[1,768,2048]{2,1,0:T(8,128)(2,1)S(1)}, bf16[1,768,2048]{2,1,0:T(8,128)(2,1)}, u32[]{:S(2)}) copy-start(bf16[1,768,2048]{2,1,0:T(8,128)(2,1)} %get-tuple-element.14) | copy-start | bytes 9437188
